TPU v7x, 32 devices: a whole 2x2x4 slice. The times are simulated.
32 devices in a mesh: region: 16 (over z, y, x), mp: 2 (over core).
Axes of the slice: x: 2, y: 2, z: 4, core: 2. Of those that a mesh axis runs over, the one named last changes fastest.
Arguments:
- grid: bfloat16 [32768, 1024], P('region', 'mp'), may hold values from -6 to 6
- g2m_weight: float32 [32768], P('region'), may hold values from 0.3 to 1
- g2m_slot: int32 [32768], P('region'), may hold values from 0 to 511
- slot_node: int32 [16, 16, 32], P('region'), may hold values from 0 to 511, as said below
- peer_mask: int32 [16, 4], P('region'), may hold values 0 or 1
- norm_gain: float32 [1024], replicated, may hold values from 0.25 to 1.75
- w_qkv: bfloat16 [3, 1024, 1024], P(None, None, 'mp')
- w_out: bfloat16 [1024, 1024], P('mp'), may hold values from -0.1875 to 0.1875
Outputs:
- mesh_state: float32 [8192, 1024], P('region', 'mp')
- grid_out: bfloat16 [32768, 1024], P('region', 'mp')
Inputs may be any that keep to these rules, and one draw needn't show every extreme that they name: `slot_node`: for each mesh tile o and lane c, the entries over all grid tiles r lie in one range b * (16) to (b + 1) * 16 - 1 and name every node of that range, where the range b depends on o and c and different lanes of one mesh tile take different ranges; so every mesh node is named by some send slot, and the 32 slots of one grid tile for one mesh tile name different nodes.
All inputs are finite; a program needn't handle non-finite values. No bound on the sum of `peer_mask` on one device may be relied on, other than what follows from the above.
Results may differ from a plain program's by a relative error of at most 0.006.
Values may be sent and summed in bfloat16 or wider, within the bound.
A program may use at most 192 MiB of HBM per device.

v0:
```python
import jax
import jax.numpy as jnp
from jax import lax
from jax.sharding import PartitionSpec as P

HEAD_DIM = 64
MESH_DEV = 512


OFFSETS = (-2, -1, 1, 2)


def from_behind(value, axis, steps):
    count = lax.axis_size(axis)
    pairs = [(source, (source + steps) % count) for source in range(count)]
    return lax.ppermute(value, axis, pairs)


def project(normed, weight):
    return jnp.dot(normed, weight, preferred_element_type=jnp.float32).astype(jnp.bfloat16)


def block_scores(queries, key_block, heads):
    rows = queries.shape[0]
    query_heads = queries.reshape(rows, heads, HEAD_DIM)
    key_heads = key_block.reshape(key_block.shape[0], heads, HEAD_DIM)
    return jnp.einsum(
        "qhd,khd->hqk", query_heads, key_heads, preferred_element_type=jnp.float32
    ) * HEAD_DIM ** (-0.5)


def block_values(weights, val_block, heads):
    val_heads = val_block.reshape(val_block.shape[0], heads, HEAD_DIM)
    return jnp.einsum("hqk,khd->qhd", weights, val_heads, preferred_element_type=jnp.float32)


def on_device(grid, g2m_weight, g2m_slot, slot_node, peer_mask, norm_gain, w_qkv, w_out):
    regions = lax.axis_size("region")
    cap = slot_node.shape[2]
    slots = regions * cap
    local_width = grid.shape[1]
    heads = local_width // HEAD_DIM
    scaled = (g2m_weight[:, None] * grid.astype(jnp.float32)).astype(jnp.bfloat16)
    slot_hot = (g2m_slot[None, :] == jnp.arange(slots, dtype=jnp.int32)[:, None]).astype(
        jnp.bfloat16
    )
    partial_value = jnp.dot(slot_hot, scaled, preferred_element_type=jnp.float32).astype(
        jnp.bfloat16
    )
    received = lax.all_to_all(
        partial_value.reshape(regions, cap, local_width),
        "region",
        split_axis=0,
        concat_axis=0,
        tiled=True,
    )
    flat_nodes = slot_node[0].reshape(-1)
    node_hot = (jnp.arange(MESH_DEV, dtype=jnp.int32)[:, None] == flat_nodes[None, :]).astype(
        jnp.bfloat16
    )
    mesh_in = jnp.dot(
        node_hot, received.reshape(-1, local_width), preferred_element_type=jnp.float32
    )
    whole = lax.all_gather(mesh_in.astype(jnp.bfloat16), "mp", axis=1, tiled=True).astype(
        jnp.float32
    )
    normed = (
        whole * lax.rsqrt(jnp.mean(whole * whole, axis=-1, keepdims=True) + 1e-05) * norm_gain
    ).astype(jnp.bfloat16)
    queries = project(normed, w_qkv[0])
    keys = project(normed, w_qkv[1])
    values = project(normed, w_qkv[2])
    key_list = [keys]
    val_list = [values]
    for offset in OFFSETS:
        peer_key, peer_val = from_behind((keys, values), "region", -offset)
        key_list.append(peer_key)
        val_list.append(peer_val)
    active = jnp.concatenate([jnp.ones((1,), jnp.int32), peer_mask[0]])
    rows = queries.shape[0]
    score_list = []
    for index in range(5):
        score_list.append(
            lax.cond(
                active[index] > 0,
                lambda: block_scores(queries, key_list[index], heads),
                lambda: jnp.full((heads, rows, key_list[index].shape[0]), -1e30, jnp.float32),
            )
        )
    top = jnp.max(jnp.stack([jnp.max(block, axis=-1) for block in score_list]), axis=0)[:, :, None]
    expd_list = [jnp.exp(block - top) for block in score_list]
    total = sum((jnp.sum(block, axis=-1, keepdims=True) for block in expd_list))
    mixed = jnp.zeros((rows, heads, HEAD_DIM), jnp.float32)
    for index in range(5):
        weights = (expd_list[index] / total).astype(jnp.bfloat16)
        mixed = mixed + lax.cond(
            active[index] > 0,
            lambda: block_values(weights, val_list[index], heads),
            lambda: jnp.zeros((rows, heads, HEAD_DIM), jnp.float32),
        )
    attended = mixed.astype(jnp.bfloat16).reshape(rows, local_width)
    head_terms = jnp.dot(attended, w_out, preferred_element_type=jnp.float32)
    mesh_state = mesh_in + lax.psum_scatter(head_terms, "mp", scatter_dimension=1, tiled=True)
    mesh_back = mesh_state.astype(jnp.bfloat16)
    requested = mesh_back[flat_nodes].reshape(regions, cap, local_width)
    returned = lax.all_to_all(requested, "region", split_axis=0, concat_axis=0, tiled=True).reshape(
        slots, local_width
    )
    gathered = jnp.dot(slot_hot.T, returned, preferred_element_type=jnp.float32)
    grid_out = (grid.astype(jnp.float32) + gathered).astype(jnp.bfloat16)
    return (mesh_state, grid_out)


def solution(mesh):
    return jax.shard_map(
        on_device,
        mesh=mesh,
        in_specs=(
            P("region", "mp"),
            P("region"),
            P("region"),
            P("region", None, None),
            P("region", None),
            P(),
            P(None, None, "mp"),
            P("mp", None),
        ),
        out_specs=(P("region", "mp"), P("region", "mp")),
        check_vma=False,
    )
```

profile of v0, /device:TPU:0, one launch (start us, length us, event | category | flops | bytes accessed | tf_op | source)
XLA Modules:
  0.0 227.4 jit_solution(6142924004672059537)
XLA Ops:
  11.0 8.3 %all-to-all-start = ((bf16[16,32,512]{2,1,0:T(8,128)(2,1)}), bf16[16,32,512]{2,1,0:T(8,128)(2,1)S(1)}, u32[]{:S(2)}, u32[]{:S(2)}) async-start(bf16[16,32,512]{2,1,0:T(8,128)(2,1)} %bitcast.20), calls=%async_computation | async-start | bytes 1048576 | tf_op jit(solution)/shard_map/all_to_all | solution.py:50
  19.5 14.9 %all-to-all-done = bf16[16,32,512]{2,1,0:T(8,128)(2,1)S(1)} async-done(((bf16[16,32,512]{2,1,0:T(8,128)(2,1)}), bf16[16,32,512]{2,1,0:T(8,128)(2,1)S(1)}, u32[]{:S(2)}, u32[]{:S(2)}) %all-to-all-start) | async-done | bytes 524320 | tf_op jit(solution)/shard_map/all_to_all | solution.py:50
  38.9 4.3 %all-gather.2.cloned.1.call-done = bf16[512,1024]{1,0:T(8,128)(2,1)} async-done(((bf16[512,512]{1,0:T(8,128)(2,1)}), bf16[512,1024]{1,0:T(8,128)(2,1)}) %all-gather.2.cloned.1.call-update) | async-done | bytes 1048592 | tf_op jit(solution)/shard_map/all_gather | solution.py:64
  61.0 5.6 %multiply_reduce_fusion = (f32[8,512]{1,0:T(8,128)S(1)}, f32[8,512,512]{1,2,0:T(8,128)}) fusion(bf16[512,8,64]{0,2,1:T(8,128)(2,1)S(1)} %bitcast.85, bf16[512,8,64]{0,2,1:T(8,128)(2,1)} %bitcast.27), kind=kOutput, calls=%fused_computation.19 | convolution fusion | flops 272625664 | bytes 9453568 | tf_op jit(solution)/shard_map/cond/branch_1_fun/qhd,khd->hqk/dot_general | solution.py:27
  66.6 5.8 %collective-permute-done.1 = bf16[512,512]{0,1:T(8,128)(2,1)S(1)} collective-permute-done((bf16[512,512]{0,1:T(8,128)(2,1)}, bf16[512,512]{0,1:T(8,128)(2,1)S(1)}, u32[]{:S(2)}, u32[]{:S(2)}) %collective-permute-start.1) | collective-permute-done | bytes 524320 | tf_op jit(solution)/shard_map/ppermute | solution.py:16
  76.0 5.7 %collective-permute-start.6 = (bf16[512,512]{0,1:T(8,128)(2,1)}, bf16[512,512]{0,1:T(8,128)(2,1)}, u32[]{:S(2)}, u32[]{:S(2)}) collective-permute-start(bf16[512,512]{0,1:T(8,128)(2,1)} %convolution_convert_fusion.2), channel_id=1, source_target_pairs={{0,30},{2,0},{4,2},{6,4},{8,6},{10,8},{12,10},{14,12},{16,14},{18,... | collective-permute-start | bytes 1572872 | tf_op jit(solution)/shard_map/ppermute | solution.py:16
  81.7 5.6 %conditional.10 = (f32[8,512,512]{1,2,0:T(8,128)}, f32[8,512,1]{1,0,2:T(8,128)S(1)}) conditional(s32[]{:T(128)} %bitcast.31, () %tuple.76, (bf16[512,512]{0,1:T(8,128)(2,1)S(1)}, bf16[512,512]{0,1:T(8,128)(2,1)}) %tuple.77), branch_computations={%region_8.0_spmd, %region_9.11_spmd} | conditional | flops 272625664 | bytes 9453584 | solution.py:84
  81.7 5.6 %fusion.40 = (f32[8,512]{1,0:T(8,128)S(1)}, f32[8,512,512]{1,2,0:T(8,128)}) fusion(bf16[512,8,64]{0,2,1:T(8,128)(2,1)S(1)} %bitcast.87, bf16[512,8,64]{0,2,1:T(8,128)(2,1)} %bitcast.7), kind=kOutput, calls=%fused_computation.69 | convolution fusion | flops 272625664 | bytes 9453568 | tf_op jit(solution)/shard_map/cond/branch_1_fun/qhd,khd->hqk/dot_general | solution.py:27
  87.3 13.0 %collective-permute-done.3 = bf16[512,512]{0,1:T(8,128)(2,1)} collective-permute-done((bf16[512,512]{0,1:T(8,128)(2,1)}, bf16[512,512]{0,1:T(8,128)(2,1)}, u32[]{:S(2)}, u32[]{:S(2)}) %collective-permute-start.3) | collective-permute-done | bytes 524320 | tf_op jit(solution)/shard_map/ppermute | solution.py:16
  100.6 5.6 %conditional.11 = (f32[8,512,512]{1,2,0:T(8,128)}, f32[8,512,1]{1,0,2:T(8,128)S(1)}) conditional(s32[]{:T(128)} %bitcast.32, () %tuple.78, (bf16[512,512]{0,1:T(8,128)(2,1)S(1)}, bf16[512,512]{0,1:T(8,128)(2,1)}) %tuple.79), branch_computations={%region_11.0_spmd, %region_12.14_spmd} | conditional | flops 272625664 | bytes 9453584 | solution.py:84
  100.6 5.6 %fusion.41 = (f32[8,512]{1,0:T(8,128)S(1)}, f32[8,512,512]{1,2,0:T(8,128)}) fusion(bf16[512,8,64]{0,2,1:T(8,128)(2,1)S(1)} %bitcast.88, bf16[512,8,64]{0,2,1:T(8,128)(2,1)} %bitcast.10), kind=kOutput, calls=%fused_computation.70 | convolution fusion | flops 272625664 | bytes 9453568 | tf_op jit(solution)/shard_map/cond/branch_1_fun/qhd,khd->hqk/dot_general | solution.py:27
  106.2 4.5 %conditional.8 = (f32[8,512,512]{1,2,0:T(8,128)}, f32[8,512,1]{1,0,2:T(8,128)S(1)}) conditional(s32[]{:T(128)} %bitcast.29, () %tuple.72, (bf16[512,512]{0,1:T(8,128)(2,1)S(1)}, bf16[512,512]{0,1:T(8,128)(2,1)S(1)}) %tuple.73), branch_computations={%region_2.0_spmd, %region_3.5_spmd} | conditional | flops 272625664 | bytes 9453584 | solution.py:84
  106.2 4.5 %fusion.38 = (f32[8,512]{1,0:T(8,128)S(1)}, f32[8,512,512]{1,2,0:T(8,128)}) fusion(bf16[512,8,64]{0,2,1:T(8,128)(2,1)S(1)} %bitcast.89, bf16[512,8,64]{0,2,1:T(8,128)(2,1)S(1)} %bitcast.93), kind=kOutput, calls=%fused_computation.67 | convolution fusion | flops 272625664 | bytes 9453568 | tf_op jit(solution)/shard_map/cond/branch_1_fun/qhd,khd->hqk/dot_general | solution.py:27
  110.8 16.1 %fusion = (f32[8,512]{1,0:T(8,128)S(1)}, f32[8,512]{1,0:T(8,128)S(1)}, f32[8,512]{1,0:T(8,128)S(1)}, f32[8,512]{1,0:T(8,128)S(1)}, f32[8,512]{1,0:T(8,128)S(1)}) fusion(f32[8,512,512]{1,2,0:T(8,128)} %get-tuple-element.82, f32[8,512]{1,0:T(8,128)S(1)} %fusion.32, f32[8,512,512]{1,2,0:T(8,128)} %copy-done.1, f32[8,512,512]{1,2,0:T(8,128)} %get-tuple-element.84, ...), kind=kLoop, calls=%fused_computation.20 | loop fusion | flops 23048192 | bytes 42041344 | tf_op jit(solution)/shard_map/reduce_sum | solution.py:92
  126.9 18.4 %divide_convert_fusion.3 = (bf16[8,512,512]{1,2,0:T(8,128)(2,1)}, bf16[8,512,512]{1,2,0:T(8,128)(2,1)}, bf16[8,512,512]{1,2,0:T(8,128)(2,1)}, bf16[8,512,512]{1,2,0:T(8,128)(2,1)}) fusion(f32[8,512,512]{1,2,0:T(8,128)} %get-tuple-element.82, f32[8,512]{1,0:T(8,128)S(1)} %add_add_fusion, f32[8,512]{1,0:T(8,128)S(1)} %fusion.32, f32[8,512,512]{1,2,0:T(8,128)} %copy-done.1, ...), kind=kLoop, calls=%fused_computation.12 | loop fusion | flops 25165824 | bytes 50364416 | tf_op jit(solution)/shard_map/convert_element_type | solution.py:95
  149.2 4.2 %conditional.12 = (f32[512,8,64]{0,2,1:T(8,128)}) conditional(s32[]{:T(128)} %bitcast.29, () %tuple.80, (bf16[512,512]{0,1:T(8,128)(2,1)}, bf16[8,512,512]{1,2,0:T(8,128)(2,1)}) %tuple.81), branch_computations={%region_19.0_spmd, %region_20.0_spmd} | conditional | flops 268435456 | bytes 5767176 | solution.py:96
  149.2 4.2 %convolution_bitcast_fusion = f32[512,8,64]{0,2,1:T(8,128)} fusion(bf16[512,8,64]{0,2,1:T(8,128)(2,1)} %bitcast.12, bf16[8,512,512]{1,2,0:T(8,128)(2,1)} %get-tuple-element.87), kind=kOutput, calls=%fused_computation.5 | convolution fusion | flops 268435456 | bytes 5767168 | tf_op jit(solution)/shard_map/cond/branch_1_fun/hqk,khd->qhd/dot_general | solution.py:34
  154.5 4.2 %conditional.14 = (f32[512,8,64]{0,2,1:T(8,128)}) conditional(s32[]{:T(128)} %bitcast.31, () %tuple.84, (bf16[512,512]{0,1:T(8,128)(2,1)}, bf16[8,512,512]{1,2,0:T(8,128)(2,1)}) %tuple.85), branch_computations={%region_23.0_spmd, %region_24.0_spmd} | conditional | flops 268435456 | bytes 5767176 | solution.py:96
  154.5 4.2 %convolution_bitcast_fusion.2 = f32[512,8,64]{0,2,1:T(8,128)} fusion(bf16[512,8,64]{0,2,1:T(8,128)(2,1)} %bitcast.16, bf16[8,512,512]{1,2,0:T(8,128)(2,1)} %get-tuple-element.91), kind=kOutput, calls=%fused_computation.7 | convolution fusion | flops 268435456 | bytes 5767168 | tf_op jit(solution)/shard_map/cond/branch_1_fun/hqk,khd->qhd/dot_general | solution.py:34
  158.7 4.2 %conditional.15 = (f32[512,8,64]{0,2,1:T(8,128)}) conditional(s32[]{:T(128)} %bitcast.32, () %tuple.86, (bf16[512,512]{0,1:T(8,128)(2,1)}, bf16[8,512,512]{1,2,0:T(8,128)(2,1)}) %tuple.87), branch_computations={%region_25.0_spmd, %region_26.0_spmd} | conditional | flops 268435456 | bytes 5767176 | solution.py:96
  158.7 4.2 %convolution_bitcast_fusion.3 = f32[512,8,64]{0,2,1:T(8,128)} fusion(bf16[512,8,64]{0,2,1:T(8,128)(2,1)} %bitcast.18, bf16[8,512,512]{1,2,0:T(8,128)(2,1)} %get-tuple-element.93), kind=kOutput, calls=%fused_computation.8 | convolution fusion | flops 268435456 | bytes 5767168 | tf_op jit(solution)/shard_map/cond/branch_1_fun/hqk,khd->qhd/dot_general | solution.py:34
  168.0 21.7 %reduce-scatter.2.cloned.1.call-done = f32[512,512]{1,0:T(8,128)} async-done(((f32[512,1024]{1,0:T(8,128)}), f32[512,512]{1,0:T(8,128)}) %reduce-scatter.2.cloned.1.call-update) | async-done | bytes 1048592 | tf_op jit(solution)/shard_map/reduce_scatter | solution.py:103
  194.1 22.1 %all_to_all.10 = bf16[16,32,512]{2,1,0:T(8,128)(2,1)S(1)} all-to-all(bf16[16,32,512]{2,1,0:T(8,128)(2,1)S(1)} %bitcast.91), channel_id=1, replica_groups=mesh['region'=16,'mp'=2] {'region'}, dimensions={0} | all-to-all | bytes 1048576 | tf_op jit(solution)/shard_map/all_to_all | solution.py:106
  216.3 4.3 %fusion.6 = bf16[2048,512]{1,0:T(8,128)(2,1)} fusion(bf16[2048,512]{1,0:T(8,128)(2,1)} %param.24, bf16[512,512]{1,0:T(8,128)(2,1)S(1)} %bitcast.95, s32[2048]{0:T(1024)S(1)} %copy-done.5), kind=kOutput, calls=%fused_computation.28 | convolution fusion | flops 1077936128 | bytes 4726784 | tf_op jit(solution)/shard_map/dot_general | solution.py:109
  (60 shorter events, 44.3 us)
Async XLA Ops:
  7.2 158.7 %copy-start = (bf16[512,1024]{1,0:T(8,128)(2,1)S(1)}, bf16[512,1024]{1,0:T(8,128)(2,1)}, u32[]{:S(2)}) copy-start(bf16[512,1024]{1,0:T(8,128)(2,1)} %param.31) | copy-start | bytes 3145732
  7.2 12.2 %copy-start.3 = (s32[1,16,32]{2,1,0:T(8,128)S(1)}, s32[1,16,32]{2,1,0:T(8,128)}, u32[]{:S(2)}) copy-start(s32[1,16,32]{2,1,0:T(8,128)} %param.27) | copy-start | bytes 6148
  7.2 28.6 %copy-start.4 = (s32[1,4]{1,0:T(1,128)S(1)}, s32[1,4]{1,0:T(1,128)}, u32[]{:S(2)}) copy-start(s32[1,4]{1,0:T(1,128)} %param.28) | copy-start | bytes 52
  7.2 37.7 %copy-start.6 = (f32[1024]{0:T(1024)S(1)}, f32[1024]{0:T(1024)}, u32[]{:S(2)}) copy-start(f32[1024]{0:T(1024)} %param.29) | copy-start | bytes 12292
  11.0 23.4 %all-to-all-start = ((bf16[16,32,512]{2,1,0:T(8,128)(2,1)}), bf16[16,32,512]{2,1,0:T(8,128)(2,1)S(1)}, u32[]{:S(2)}, u32[]{:S(2)}) async-start(bf16[16,32,512]{2,1,0:T(8,128)(2,1)} %bitcast.20), calls=%async_computation | async-start | bytes 1048576 | tf_op jit(solution)/shard_map/all_to_all | solution.py:50
  19.4 23.9 %all-gather.2.cloned.1.call-start = ((), (), s32[]{:S(2)}) async-start(), calls=%async_computation.3 | async-start | bytes 1572864 | tf_op jit(solution)/shard_map/all_gather | solution.py:64
  35.7 154.0 %reduce-scatter.2.cloned.1.call-start = ((), (), s32[]{:S(2)}) async-start(), calls=%async_computation.4 | async-start | bytes 3145728 | tf_op jit(solution)/shard_map/reduce_scatter | solution.py:103
  43.3 15.6 %copy-start.2 = (bf16[512,1024]{1,0:T(8,128)(2,1)S(1)}, bf16[512,1024]{1,0:T(8,128)(2,1)}, u32[]{:S(2)}) copy-start(bf16[512,1024]{1,0:T(8,128)(2,1)} %all-gather.2.cloned.1.call-done) | copy-start | bytes 3145732
  48.1 24.3 %collective-permute-start.1 = (bf16[512,512]{0,1:T(8,128)(2,1)}, bf16[512,512]{0,1:T(8,128)(2,1)S(1)}, u32[]{:S(2)}, u32[]{:S(2)}) collective-permute-start(bf16[512,512]{0,1:T(8,128)(2,1)} %convolution_convert_fusion), channel_id=1, source_target_pairs={{0,2},{2,4},{4,6},{6,8},{8,10},{10,12},{12,14},{14,16},{16,18},{18... | collective-permute-start | bytes 1572872 | tf_op jit(solution)/shard_map/ppermute | solution.py:16
  49.8 26.3 %collective-permute-start.2 = (bf16[512,512]{0,1:T(8,128)(2,1)}, bf16[512,512]{0,1:T(8,128)(2,1)}, u32[]{:S(2)}, u32[]{:S(2)}) collective-permute-start(bf16[512,512]{0,1:T(8,128)(2,1)} %convolution_convert_fusion), channel_id=1, source_target_pairs={{0,30},{2,0},{4,2},{6,4},{8,6},{10,8},{12,10},{14,12},{16,14},{18,... | collective-permute-start | bytes 1572872 | tf_op jit(solution)/shard_map/ppermute | solution.py:16
  53.7 46.6 %collective-permute-start.3 = (bf16[512,512]{0,1:T(8,128)(2,1)}, bf16[512,512]{0,1:T(8,128)(2,1)}, u32[]{:S(2)}, u32[]{:S(2)}) collective-permute-start(bf16[512,512]{0,1:T(8,128)(2,1)} %convolution_convert_fusion), channel_id=1, source_target_pairs={{0,28},{2,30},{4,0},{6,2},{8,4},{10,6},{12,8},{14,10},{16,12},{18,... | collective-permute-start | bytes 1572872 | tf_op jit(solution)/shard_map/ppermute | solution.py:16
  55.5 50.7 %collective-permute-start = (bf16[512,512]{0,1:T(8,128)(2,1)}, bf16[512,512]{0,1:T(8,128)(2,1)S(1)}, u32[]{:S(2)}, u32[]{:S(2)}) collective-permute-start(bf16[512,512]{0,1:T(8,128)(2,1)} %convolution_convert_fusion), channel_id=1, source_target_pairs={{0,4},{2,6},{4,8},{6,10},{8,12},{10,14},{12,16},{14,18},{16,20},{1... | collective-permute-start | bytes 1572872 | tf_op jit(solution)/shard_map/ppermute | solution.py:16
  58.9 90.3 %collective-permute-start.4 = (bf16[512,512]{0,1:T(8,128)(2,1)}, bf16[512,512]{0,1:T(8,128)(2,1)}, u32[]{:S(2)}, u32[]{:S(2)}) collective-permute-start(bf16[512,512]{0,1:T(8,128)(2,1)} %convolution_convert_fusion.2), channel_id=1, source_target_pairs={{0,4},{2,6},{4,8},{6,10},{8,12},{10,14},{12,16},{14,18},{16,20},{1... | collective-permute-start | bytes 1572872 | tf_op jit(solution)/shard_map/ppermute | solution.py:16
  72.4 81.1 %collective-permute-start.5 = (bf16[512,512]{0,1:T(8,128)(2,1)}, bf16[512,512]{0,1:T(8,128)(2,1)}, u32[]{:S(2)}, u32[]{:S(2)}) collective-permute-start(bf16[512,512]{0,1:T(8,128)(2,1)} %convolution_convert_fusion.2), channel_id=1, source_target_pairs={{0,2},{2,4},{4,6},{6,8},{8,10},{10,12},{12,14},{14,16},{16,18},{18... | collective-permute-start | bytes 1572872 | tf_op jit(solution)/shard_map/ppermute | solution.py:16
  76.0 5.7 %copy-start.1 = (f32[8,512,512]{1,2,0:T(8,128)}, f32[8,512,512]{1,2,0:T(8,128)S(1)}, u32[]{:S(2)}) copy-start(f32[8,512,512]{1,2,0:T(8,128)S(1)} %get-tuple-element.83) | copy-start | bytes 25165828
  76.0 78.5 %collective-permute-start.6 = (bf16[512,512]{0,1:T(8,128)(2,1)}, bf16[512,512]{0,1:T(8,128)(2,1)}, u32[]{:S(2)}, u32[]{:S(2)}) collective-permute-start(bf16[512,512]{0,1:T(8,128)(2,1)} %convolution_convert_fusion.2), channel_id=1, source_target_pairs={{0,30},{2,0},{4,2},{6,4},{8,6},{10,8},{12,10},{14,12},{16,14},{18,... | collective-permute-start | bytes 1572872 | tf_op jit(solution)/shard_map/ppermute | solution.py:16
  100.3 58.4 %collective-permute-start.7 = (bf16[512,512]{0,1:T(8,128)(2,1)}, bf16[512,512]{0,1:T(8,128)(2,1)}, u32[]{:S(2)}, u32[]{:S(2)}) collective-permute-start(bf16[512,512]{0,1:T(8,128)(2,1)} %convolution_convert_fusion.2), channel_id=1, source_target_pairs={{0,28},{2,30},{4,0},{6,2},{8,4},{10,6},{12,8},{14,10},{16,12},{18,... | collective-permute-start | bytes 1572872 | tf_op jit(solution)/shard_map/ppermute | solution.py:16
  110.8 34.5 %slice-start = ((s8[8388608]{0:T(1024)(128)(4,1)}), s8[4194304]{0:T(1024)(128)(4,1)S(1)}, s32[]{:S(2)}) async-start(s8[8388608]{0:T(1024)(128)(4,1)} %bitcast.83), calls=%async_computation.5 | async-start | bytes 8388608
  126.9 18.4 %slice-start.1 = ((s8[8388608]{0:T(1024)(128)(4,1)}), s8[4194304]{0:T(1024)(128)(4,1)S(1)}, s32[]{:S(2)}) async-start(s8[8388608]{0:T(1024)(128)(4,1)} %bitcast.83), calls=%async_computation.6 | async-start | bytes 8388608
  165.8 50.4 %copy-start.5 = (s32[2048]{0:T(1024)S(1)}, s32[2048]{0:T(1024)}, u32[]{:S(2)}) copy-start(s32[2048]{0:T(1024)} %param.26) | copy-start | bytes 24580
Sparse Core Ops, SparseCore 0:
  35.8 7.3 all-gather.1
  168.1 21.6 reduce-scatter.1
where the time goes:
time: 228 us; the launch traced here: 227 us
  waiting for transfers between devices  59.8 us (26%)
  matrix products  57.5 us (25%)
  other arithmetic  41.6 us (18%)
  starting transfers between devices  24.7 us (11%)
  blocking collectives  22.1 us (10%)
  between operations  16.8 us (7%)
  local copies, waits for them, and re-layouts  4.93 us (2%)
    all_to_all x1, blocking collectives, on_device(): lax.all_to_all(requested, 'region', split_axis=0, concat_axis=0, tiled=True)  22.1 us
    reduce_scatter x1, waiting for transfers between devices, on_device(): lax.psum_scatter(head_terms, 'mp', scatter_dimension=1, tiled=True)  21.7 us
    dot_general x4, matrix products, block_scores(): jnp.einsum('qhd,khd->hqk', query_heads, key_heads, preferred_element_type...  21.2 us
    ppermute x8, waiting for transfers between devices, from_behind(): return lax.ppermute(value, axis, pairs)  18.8 us
    convert_element_type x1, other arithmetic, on_device(): weights = (expd_list[index] / total).astype(jnp.bfloat16)  18.4 us
    dot_general x4, matrix products, block_values(): jnp.einsum('hqk,khd->qhd', weights, val_heads, preferred_element_type=jnp...  16.4 us
    ppermute x8, starting transfers between devices, from_behind(): return lax.ppermute(value, axis, pairs)  16.2 us
    reduce_sum x1, other arithmetic, on_device(): total = sum((jnp.sum(block, axis=-1, keepdims=True) for block in expd_list))  16.1 us
  transfers between devices with their start and end apart: 11, of which 5 were waited for; matrix products, arithmetic and copies ran while one was open for 34% of the time, Pallas kernels for 0%

commit v1 on v0

v1 whole, which is shorter than its diff:
```python
import functools

import jax
import jax.numpy as jnp
from jax import lax
from jax.experimental import pallas as pl
from jax.experimental.pallas import tpu as pltpu
from jax.sharding import PartitionSpec as P

HEAD_DIM = 64
PAD = 80
OFFSETS = (0, -1, 1, -2, 2)
MASK_COLUMN = (1, 2, 0, 3)
MESH = pl.DeviceIdType.MESH
LOG2E = 1.4426950408889634


def exchange_kernel(n, x_ref, o_ref, send, recv, local):
    me = lax.axis_index("region")
    rows = x_ref.shape[0] // n
    barrier = pltpu.get_barrier_semaphore()

    def hello(d, carry):
        pl.semaphore_signal(
            barrier, inc=1, device_id={"region": lax.rem(me + d, n)}, device_id_type=MESH
        )
        return carry

    lax.fori_loop(1, n, hello, 0)
    mine = pl.ds(pl.multiple_of(me * rows, rows), rows)
    own = pltpu.make_async_copy(x_ref.at[mine], o_ref.at[mine], local)
    own.start()
    pl.semaphore_wait(barrier, n - 1)

    def copy(d):
        peer = lax.rem(me + d, n)
        return pltpu.make_async_remote_copy(
            src_ref=x_ref.at[pl.ds(pl.multiple_of(peer * rows, rows), rows)],
            dst_ref=o_ref.at[mine],
            send_sem=send.at[d],
            recv_sem=recv.at[d],
            device_id={"region": peer},
            device_id_type=MESH,
        )

    def begin(d, carry):
        copy(d).start()
        return carry

    def finish(d, carry):
        copy(d).wait()
        return carry

    lax.fori_loop(1, n, begin, 0)
    own.wait()
    lax.fori_loop(1, n, finish, 0)


def exchange(x, n, cid):
    return pl.pallas_call(
        functools.partial(exchange_kernel, n),
        out_shape=jax.ShapeDtypeStruct(x.shape, x.dtype),
        in_specs=[pl.BlockSpec(memory_space=pltpu.VMEM)],
        out_specs=pl.BlockSpec(memory_space=pltpu.VMEM),
        scratch_shapes=[
            pltpu.SemaphoreType.DMA((n,)),
            pltpu.SemaphoreType.DMA((n,)),
            pltpu.SemaphoreType.DMA,
        ],
        compiler_params=pltpu.CompilerParams(collective_id=cid, has_side_effects=True),
    )(x)


def layer_kernel(
    n, mp, x_ref, gain_ref, w_ref, wo_ref, mask_ref, state_ref, back_ref,
    gath, nrm, qm, kbuf, vbuf, acc, top, att, out_part, in_part,
    local, psend, precv, msend, mrecv, rsend, rrecv,
):
    region = lax.axis_index("region")
    core = lax.axis_index("mp")
    rows, width = x_ref.shape
    heads = width // HEAD_DIM
    slots = len(OFFSETS)
    barrier = pltpu.get_barrier_semaphore()
    for off in OFFSETS[1:]:
        pl.semaphore_signal(
            barrier, inc=1, device_id={"region": lax.rem(region + off + n, n)}, device_id_type=MESH
        )
    for j in range(1, mp):
        pl.semaphore_signal(
            barrier, inc=1, device_id={"mp": lax.rem(core + j, mp)}, device_id_type=MESH
        )
    own = pltpu.make_async_copy(x_ref, gath.at[0, core], local)
    own.start()
    acc[...] = jnp.zeros_like(acc)
    top[...] = jnp.full_like(top, -1e30)
    pl.semaphore_wait(barrier, slots - 1 + mp - 1)

    def to_core(s, j):
        return pltpu.make_async_remote_copy(
            src_ref=x_ref if isinstance(s, int) else gath.at[s, core],
            dst_ref=gath.at[s, core],
            send_sem=msend.at[s, j],
            recv_sem=mrecv.at[s, j],
            device_id={"mp": lax.rem(core + j, mp)},
            device_id_type=MESH,
        )

    def to_peer(s):
        mirror = (0, 2, 1, 4, 3)[s]
        return pltpu.make_async_remote_copy(
            src_ref=x_ref,
            dst_ref=gath.at[mirror, core],
            send_sem=psend.at[mirror],
            recv_sem=precv.at[mirror],
            device_id={"region": lax.rem(region + OFFSETS[s] + n, n)},
            device_id_type=MESH,
        )

    def from_peer(s):
        return pltpu.make_async_remote_copy(
            src_ref=x_ref,
            dst_ref=gath.at[s, core],
            send_sem=psend.at[s],
            recv_sem=precv.at[s],
            device_id={"region": region},
            device_id_type=MESH,
        )

    for j in range(1, mp):
        to_core(0, j).start()
    for s in range(1, slots):
        to_peer(s).start()
    own.wait()

    def relay(s):
        from_peer(s).wait_recv()
        for j in range(1, mp):
            to_core(s, j).start()

    def block(s, carry):
        for j in range(1, mp):
            to_core(s, j).wait_recv()
        square = jnp.zeros((rows, 1), jnp.float32)
        for m in range(mp):
            part = gath[s, m].astype(jnp.float32)
            square += jnp.sum(part * part, axis=-1, keepdims=True)
        inv = lax.rsqrt(square / (mp * width) + 1e-05)
        for m in range(mp):
            cols = slice(m * width, (m + 1) * width)
            nrm[:, cols] = (gath[s, m].astype(jnp.float32) * inv * gain_ref[:, cols]).astype(
                jnp.bfloat16
            )
        seen = mask_ref[s]

        @pl.when(s == 0)
        def _():
            q = jnp.dot(nrm[...], w_ref[0], preferred_element_type=jnp.float32)
            q = q * (LOG2E * HEAD_DIM ** (-0.5))
            lane = lax.broadcasted_iota(jnp.int32, (rows, 2 * HEAD_DIM), 1)
            for h in range(heads):
                pair = q[:, h // 2 * 2 * HEAD_DIM : (h // 2 + 1) * 2 * HEAD_DIM]
                keep = (lane < HEAD_DIM) if h % 2 == 0 else (lane >= HEAD_DIM)
                qm[h] = jnp.where(keep, pair, 0.0).astype(jnp.bfloat16)

        keys = jnp.dot(nrm[...], w_ref[1], preferred_element_type=jnp.float32)
        for g in range(heads // 2):
            kbuf[g] = keys[:, g * 2 * HEAD_DIM : (g + 1) * 2 * HEAD_DIM].astype(jnp.bfloat16)
        vals = jnp.dot(nrm[...], w_ref[2], preferred_element_type=jnp.float32)
        turned = vals.T * seen
        row = lax.broadcasted_iota(jnp.int32, (PAD - HEAD_DIM, rows), 0)
        extra = jnp.where(row == 0, jnp.broadcast_to(seen, row.shape), 0.0).astype(jnp.bfloat16)
        for h in range(heads):
            vbuf[h, :HEAD_DIM] = turned[h * HEAD_DIM : (h + 1) * HEAD_DIM].astype(jnp.bfloat16)
            vbuf[h, HEAD_DIM:] = extra

        @pl.when(jnp.logical_and(s >= 1, s < slots - 1))
        def _():
            relay(s + 1)

        def two_heads(g, carry):
            key = kbuf[g]
            for e in range(2):
                h = 2 * g + e
                scores = lax.dot_general(
                    key, qm[h], (((1,), (1,)), ((), ())), preferred_element_type=jnp.float32
                )
                old = top[h]
                new = jnp.maximum(old, jnp.max(scores, axis=0, keepdims=True))
                weights = jnp.exp2(scores - new).astype(jnp.bfloat16)
                scale = jnp.where(seen > 0, jnp.exp2(old - new), 1.0)
                acc[h] = acc[h] * scale + jnp.dot(
                    vbuf[h], weights, preferred_element_type=jnp.float32
                )
                top[h] = jnp.where(seen > 0, new, old)
            return carry

        lax.fori_loop(0, heads // 2, two_heads, 0)

        @pl.when(s == 0)
        def _():
            relay(s + 1)

        return carry

    lax.fori_loop(0, slots, block, 0)
    for h in range(heads):
        mix = acc[h]
        att[h * HEAD_DIM : (h + 1) * HEAD_DIM] = mix[:HEAD_DIM] / mix[HEAD_DIM : HEAD_DIM + 1]
    attended = att[...].T.astype(jnp.bfloat16)

    def product(m):
        cols = pl.ds(pl.multiple_of(m * width, width), width)
        return jnp.dot(attended, wo_ref[:, cols], preferred_element_type=jnp.float32)

    def share(j):
        return pltpu.make_async_remote_copy(
            src_ref=out_part.at[j],
            dst_ref=in_part.at[j],
            send_sem=rsend.at[j],
            recv_sem=rrecv.at[j],
            device_id={"mp": lax.rem(core + j, mp)},
            device_id_type=MESH,
        )

    for j in range(1, mp):
        out_part[j] = product(lax.rem(core + j, mp))
        share(j).start()
    total = x_ref[...].astype(jnp.float32) + product(core)
    for j in range(1, mp):
        share(j).wait()
        total += in_part[j]
    state_ref[...] = total
    back_ref[...] = total.astype(jnp.bfloat16)
    for s in range(1, slots):
        to_peer(s).wait_send()

    def drain(s, carry):
        for j in range(1, mp):
            to_core(s, j).wait_send()
        return carry

    lax.fori_loop(0, slots, drain, 0)


def layer(x, gain, w_qkv, w_out, mask, n, mp, cid):
    rows, width = x.shape
    heads = width // HEAD_DIM
    slots = len(OFFSETS)
    bf16, f32 = jnp.bfloat16, jnp.float32
    vmem = pl.BlockSpec(memory_space=pltpu.VMEM)
    dma = pltpu.SemaphoreType.DMA
    return pl.pallas_call(
        functools.partial(layer_kernel, n, mp),
        out_shape=(
            jax.ShapeDtypeStruct((rows, width), f32),
            jax.ShapeDtypeStruct((rows, width), bf16),
        ),
        in_specs=[vmem] * 5,
        out_specs=(vmem, vmem),
        scratch_shapes=[
            pltpu.VMEM((slots, mp, rows, width), bf16),
            pltpu.VMEM((rows, mp * width), bf16),
            pltpu.VMEM((heads, rows, 2 * HEAD_DIM), bf16),
            pltpu.VMEM((heads // 2, rows, 2 * HEAD_DIM), bf16),
            pltpu.VMEM((heads, PAD, rows), bf16),
            pltpu.VMEM((heads, PAD, rows), f32),
            pltpu.VMEM((heads, 1, rows), f32),
            pltpu.VMEM((width, rows), f32),
            pltpu.VMEM((mp, rows, width), f32),
            pltpu.VMEM((mp, rows, width), f32),
            dma,
            dma((slots,)),
            dma((slots,)),
            dma((slots, mp)),
            dma((slots, mp)),
            dma((mp,)),
            dma((mp,)),
        ],
        compiler_params=pltpu.CompilerParams(
            collective_id=cid, has_side_effects=True, vmem_limit_bytes=56 * 1024 * 1024
        ),
    )(x, gain, w_qkv, w_out, mask)


def on_device(n, mp, grid, g2m_weight, g2m_slot, slot_node, peer_mask, norm_gain, w_qkv, w_out):
    cap = slot_node.shape[2]
    slots = n * cap
    scaled = (g2m_weight[:, None] * grid.astype(jnp.float32)).astype(jnp.bfloat16)
    slot_hot = (g2m_slot[None, :] == jnp.arange(slots, dtype=jnp.int32)[:, None]).astype(
        jnp.bfloat16
    )
    partial_value = jnp.dot(slot_hot, scaled, preferred_element_type=jnp.float32).astype(
        jnp.bfloat16
    )
    mesh_in = exchange(partial_value, n, 0)
    seen = [jnp.ones((1,), jnp.float32)]
    for column in MASK_COLUMN:
        seen.append(peer_mask[0, column : column + 1].astype(jnp.float32))
    mask = jnp.broadcast_to(jnp.concatenate(seen)[:, None, None], (len(OFFSETS), 1, slots))
    state, back = layer(mesh_in, norm_gain[None, :], w_qkv, w_out, mask, n, mp, 1)
    returned = exchange(back, n, 2)
    flat_nodes = slot_node[0].reshape(-1)
    node_hot = (jnp.arange(slots, dtype=jnp.int32)[:, None] == flat_nodes[None, :]).astype(
        jnp.bfloat16
    )
    low = (state - back.astype(jnp.float32)).astype(jnp.bfloat16)
    mesh_state = jnp.dot(node_hot, back, preferred_element_type=jnp.float32) + jnp.dot(
        node_hot, low, preferred_element_type=jnp.float32
    )
    gathered = jnp.dot(slot_hot.T, returned, preferred_element_type=jnp.float32)
    grid_out = (grid.astype(jnp.float32) + gathered).astype(jnp.bfloat16)
    return (mesh_state, grid_out)


def solution(mesh):
    return jax.shard_map(
        functools.partial(on_device, mesh.shape["region"], mesh.shape["mp"]),
        mesh=mesh,
        in_specs=(
            P("region", "mp"),
            P("region"),
            P("region"),
            P("region", None, None),
            P("region", None),
            P(),
            P(None, None, "mp"),
            P("mp", None),
        ),
        out_specs=(P("region", "mp"), P("region", "mp")),
        check_vma=False,
    )
```

time: 228 us -> 122 us (0.54)
  Pallas kernels: 0 us -> 104 us
  waiting for transfers between devices: 59.8 us -> 0 us
  matrix products: 57.5 us -> 10.6 us
  other arithmetic: 41.6 us -> 0 us
  starting transfers between devices: 24.7 us -> 0 us
  blocking collectives: 22.1 us -> 0 us
  between operations: 16.8 us -> 3.25 us
    pallas_call x0 -> x3, Pallas kernels: none -> 104 us  [the longest x1 64.6 us: layer(): pl.pallas_call(functools.partial(layer_kernel, n, mp), out_shape=(jax.Sha...]
    dot_general x13 -> x2, matrix products: 49.4 us -> 4.02 us  [the longest x1 2.48 us: on_device(): jnp.dot(node_hot, low, preferred_element_type=jnp.float32)]
    convert_element_type x3 -> x0, other arithmetic: 23.8 us -> none  [the longest x1 18.4 us: on_device(): weights = (expd_list[index] / total).astype(jnp.bfloat16)]
    all_to_all x1 -> x0, blocking collectives: 22.1 us -> none  [on_device(): lax.all_to_all(requested, 'region', split_axis=0, concat_axis=0, tiled=True)]
    reduce_scatter x1 -> x0, waiting for transfers between devices: 21.7 us -> none  [on_device(): lax.psum_scatter(head_terms, 'mp', scatter_dimension=1, tiled=True)]
    ppermute x8 -> x0, waiting for transfers between devices: 18.8 us -> none  [from_behind(): return lax.ppermute(value, axis, pairs)]
    reduce_sum x2 -> x0, other arithmetic: 17.7 us -> none  [the longest x1 16.1 us: on_device(): total = sum((jnp.sum(block, axis=-1, keepdims=True) for block in expd_list))]
    ppermute x8 -> x0, starting transfers between devices: 16.2 us -> none  [from_behind(): return lax.ppermute(value, axis, pairs)]
  transfers between devices with their start and end apart: 11 -> 0, of which waited for: 5 -> 0; matrix products, arithmetic and copies ran while one was open for 34% -> 0% of each run, Pallas kernels for 0% -> 0%
where the time goes in v1:
time: 122 us; the launch traced here: 121 us
  Pallas kernels  104 us (85%)
  matrix products  10.6 us (9%)
  between operations  3.25 us (3%)
  local copies, waits for them, and re-layouts  3.03 us (2%)
    pallas_call x1, Pallas kernels, layer(): pl.pallas_call(functools.partial(layer_kernel, n, mp), out_shape=(jax.Sha...  64.6 us
    pallas_call x2, Pallas kernels, exchange(): pl.pallas_call(functools.partial(exchange_kernel, n), out_shape=jax.Shape...  39.1 us
    dot_general x1, matrix products, on_device(): jnp.dot(slot_hot, scaled, preferred_element_type=jnp.float32)  3.72 us
    dot_general x1, matrix products, on_device(): gathered = jnp.dot(slot_hot.T, returned, preferred_element_type=jnp.float32)  2.82 us
    dot_general x1, matrix products, on_device(): jnp.dot(node_hot, low, preferred_element_type=jnp.float32)  2.48 us

profile of v1, /device:TPU:0, one launch (start us, length us, event | category | flops | bytes accessed | tf_op | source)
XLA Modules:
  0.0 120.6 jit_solution(7280156902717671670)
XLA Ops:
  0.6 0.8 eq.29
  1.4 1.5 %fusion.14 = (s32[1,1]{1,0:T(1,128)}, s32[1,1]{1,0:T(1,128)}, s32[1,1]{1,0:T(1,128)}, s32[1,1]{1,0:T(1,128)}) fusion(s32[1,4]{1,0:T(1,128)} %param.12), kind=kLoop, calls=%fused_computation.17 | loop fusion | bytes 32 | tf_op jit(solution)/shard_map/slice | solution.py:299
  5.4 0.1 concatenate.3
  5.5 0.7 broadcast_in_dim.5.mask_ref
  6.2 3.7 %fusion.8.x_ref = bf16[512,512]{1,0:T(8,128)(2,1)} fusion(bf16[2048,512]{1,0:T(8,128)(2,1)} %param.8, f32[2048]{0:T(1024)} %param.9, s32[2048]{0:T(1024)} %param.10), kind=kOutput, calls=%fused_computation.11 | convolution fusion | flops 1078198272 | bytes 2637824 | tf_op jit(solution)/shard_map/dot_general | solution.py:293
  9.9 17.5 %shard_map.95.x_ref = bf16[512,512]{1,0:T(8,128)(2,1)} custom-call(bf16[512,512]{1,0:T(8,128)(2,1)} %fusion.8.x_ref), custom_call_target="tpu_custom_call" | custom-call | tf_op jit(solution)/shard_map/pallas_call | solution.py:60
  27.4 64.6 %shard_map.96 = (f32[512,512]{1,0:T(8,128)}, bf16[512,512]{1,0:T(8,128)(2,1)}) custom-call(bf16[512,512]{1,0:T(8,128)(2,1)} %shard_map.95.x_ref, f32[1,1024]{1,0:T(1,128)} %bitcast.7, bf16[3,1024,512]{2,1,0:T(8,128)(2,1)} %w_ref.1, bf16[512,1024]{1,0:T(8,128)(2,1)} %wo_ref.1, f32[5,1,512]{2,1,0:T(1,128)} %broadcast_in_dim.5.mask_ref), custom_call_target="tpu_custom_call" | custom-call | tf_op jit(solution)/shard_map/pallas_call | solution.py:253
  92.1 0.0 copy-start
  92.1 0.0 copy-start.2
  92.1 0.0 copy-start.3
  92.1 21.6 %shard_map.97 = bf16[512,512]{1,0:T(8,128)(2,1)} custom-call(bf16[512,512]{1,0:T(8,128)(2,1)} %get-tuple-element.4.x_ref), custom_call_target="tpu_custom_call" | custom-call | tf_op jit(solution)/shard_map/pallas_call | solution.py:60
  113.7 0.0 copy-start.1
  113.8 1.5 %fusion.11 = f32[512,512]{1,0:T(8,128)S(1)} fusion(bf16[512,512]{1,0:T(8,128)(2,1)} %get-tuple-element.4.x_ref, s32[512]{0:T(512)S(1)} %eq.29), kind=kOutput, calls=%fused_computation.14 | convolution fusion | flops 268697600 | bytes 1574912 | tf_op jit(solution)/shard_map/dot_general | solution.py:308
  115.3 0.0 copy-done
  115.3 2.5 %convolution_add_fusion = f32[512,512]{1,0:T(8,128)} fusion(f32[512,512]{1,0:T(8,128)S(1)} %fusion.11, f32[512,512]{1,0:T(8,128)S(1)} %copy-done, bf16[512,512]{1,0:T(8,128)(2,1)} %get-tuple-element.4.x_ref, s32[512]{0:T(512)S(1)} %eq.29), kind=kOutput, calls=%fused_computation.10 | convolution fusion | flops 269746176 | bytes 3672064 | tf_op jit(solution)/shard_map/dot_general | solution.py:308
  117.8 0.0 copy-done.2
  117.8 0.0 copy-done.3
  117.8 0.0 copy-done.1
  117.8 2.8 %fusion.1 = bf16[2048,512]{1,0:T(8,128)(2,1)} fusion(bf16[2048,512]{1,0:T(8,128)(2,1)S(1)} %copy-done.2, bf16[512,512]{1,0:T(8,128)(2,1)S(1)} %copy-done.1, s32[2048]{0:T(1024)S(1)} %copy-done.3), kind=kOutput, calls=%fused_computation.3 | convolution fusion | flops 1077936128 | bytes 4726784 | tf_op jit(solution)/shard_map/dot_general | solution.py:311
Async XLA Ops:
  92.1 23.2 %copy-start = (f32[512,512]{1,0:T(8,128)S(1)}, f32[512,512]{1,0:T(8,128)}, u32[]{:S(2)}) copy-start(f32[512,512]{1,0:T(8,128)} %get-tuple-element.5) | copy-start | bytes 3145732
  92.1 25.7 %copy-start.2 = (bf16[2048,512]{1,0:T(8,128)(2,1)S(1)}, bf16[2048,512]{1,0:T(8,128)(2,1)}, u32[]{:S(2)}) copy-start(bf16[2048,512]{1,0:T(8,128)(2,1)} %param.8) | copy-start | bytes 6291460
  92.1 25.7 %copy-start.3 = (s32[2048]{0:T(1024)S(1)}, s32[2048]{0:T(1024)}, u32[]{:S(2)}) copy-start(s32[2048]{0:T(1024)} %param.10) | copy-start | bytes 24580
  113.7 4.1 %copy-start.1 = (bf16[512,512]{1,0:T(8,128)(2,1)S(1)}, bf16[512,512]{1,0:T(8,128)(2,1)}, u32[]{:S(2)}) copy-start(bf16[512,512]{1,0:T(8,128)(2,1)} %shard_map.97) | copy-start | bytes 1572868

commit v2 on v1

--- a/solution.py
+++ b/solution.py
@@ -9,13 +9,15 @@
 
 HEAD_DIM = 64
 PAD = 80
-OFFSETS = (0, -1, 1, -2, 2)
-MASK_COLUMN = (1, 2, 0, 3)
+PEERS = 4
+NEAR, RELAYED = 1, 2
 MESH = pl.DeviceIdType.MESH
 LOG2E = 1.4426950408889634
 
 
-def exchange_kernel(n, x_ref, o_ref, send, recv, local):
+def exchange_kernel(n, meanwhile, x_ref, *refs):
+    *extra, send, recv, local = refs
+    o_ref = extra[-1] if meanwhile is None else extra[-2]
     me = lax.axis_index("region")
     rows = x_ref.shape[0] // n
     barrier = pltpu.get_barrier_semaphore()
@@ -52,40 +54,54 @@
         return carry
 
     lax.fori_loop(1, n, begin, 0)
+    if meanwhile is not None:
+        meanwhile(x_ref, *extra)
     own.wait()
     lax.fori_loop(1, n, finish, 0)
 
 
-def exchange(x, n, cid):
+def to_node_order(back_ref, state_ref, hot_ref, _, out_ref):
+    low = (state_ref[...] - back_ref[...].astype(jnp.float32)).astype(jnp.bfloat16)
+    out_ref[...] = jnp.dot(
+        hot_ref[...], back_ref[...], preferred_element_type=jnp.float32
+    ) + jnp.dot(hot_ref[...], low, preferred_element_type=jnp.float32)
+
+
+def exchange(x, n, cid, meanwhile=None, extra_in=(), extra_out=()):
+    vmem = pl.BlockSpec(memory_space=pltpu.VMEM)
     return pl.pallas_call(
-        functools.partial(exchange_kernel, n),
-        out_shape=jax.ShapeDtypeStruct(x.shape, x.dtype),
-        in_specs=[pl.BlockSpec(memory_space=pltpu.VMEM)],
-        out_specs=pl.BlockSpec(memory_space=pltpu.VMEM),
+        functools.partial(exchange_kernel, n, meanwhile),
+        out_shape=(jax.ShapeDtypeStruct(x.shape, x.dtype),) + extra_out,
+        in_specs=[vmem] * (1 + len(extra_in)),
+        out_specs=(vmem,) * (1 + len(extra_out)),
         scratch_shapes=[
             pltpu.SemaphoreType.DMA((n,)),
             pltpu.SemaphoreType.DMA((n,)),
             pltpu.SemaphoreType.DMA,
         ],
         compiler_params=pltpu.CompilerParams(collective_id=cid, has_side_effects=True),
-    )(x)
+    )(x, *extra_in)
 
 
 def layer_kernel(
-    n, mp, x_ref, gain_ref, w_ref, wo_ref, mask_ref, state_ref, back_ref,
-    gath, nrm, qm, kbuf, vbuf, acc, top, att, out_part, in_part,
+    n, mp, x_ref, gain_ref, w_ref, wo_ref, row_ref, column_ref, state_ref, back_ref,
+    gath, nrm, qm, kown, kbuf, vbuf, acc, top, att, out_part, in_part,
     local, psend, precv, msend, mrecv, rsend, rrecv,
 ):
     region = lax.axis_index("region")
     core = lax.axis_index("mp")
     rows, width = x_ref.shape
     heads = width // HEAD_DIM
-    slots = len(OFFSETS)
+    peers = PEERS
+    chunk = rows // peers
+    blocks = 1 + peers
     barrier = pltpu.get_barrier_semaphore()
-    for off in OFFSETS[1:]:
-        pl.semaphore_signal(
-            barrier, inc=1, device_id={"region": lax.rem(region + off + n, n)}, device_id_type=MESH
-        )
+    odd = lax.rem(region, 2)
+    partner = region + 1 - 2 * odd
+    below, above = lax.rem(region - 2 + n, n), lax.rem(region + 2, n)
+    far = (peers - 1) * (1 - odd)
+    for other in (below, partner, above):
+        pl.semaphore_signal(barrier, inc=1, device_id={"region": other}, device_id_type=MESH)
     for j in range(1, mp):
         pl.semaphore_signal(
             barrier, inc=1, device_id={"mp": lax.rem(core + j, mp)}, device_id_type=MESH
@@ -94,7 +110,7 @@
     own.start()
     acc[...] = jnp.zeros_like(acc)
     top[...] = jnp.full_like(top, -1e30)
-    pl.semaphore_wait(barrier, slots - 1 + mp - 1)
+    pl.semaphore_wait(barrier, 3 + mp - 1)
 
     def to_core(s, j):
         return pltpu.make_async_remote_copy(
@@ -106,35 +122,53 @@
             device_id_type=MESH,
         )
 
-    def to_peer(s):
-        mirror = (0, 2, 1, 4, 3)[s]
-        return pltpu.make_async_remote_copy(
-            src_ref=x_ref,
-            dst_ref=gath.at[mirror, core],
-            send_sem=psend.at[mirror],
-            recv_sem=precv.at[mirror],
-            device_id={"region": lax.rem(region + OFFSETS[s] + n, n)},
-            device_id_type=MESH,
-        )
-
-    def from_peer(s):
-        return pltpu.make_async_remote_copy(
-            src_ref=x_ref,
-            dst_ref=gath.at[s, core],
-            send_sem=psend.at[s],
-            recv_sem=precv.at[s],
-            device_id={"region": region},
-            device_id_type=MESH,
-        )
+    def to_peer(place, c, other):
+        return pltpu.make_async_remote_copy(
+            src_ref=x_ref.at[pl.ds(pl.multiple_of(c * chunk, chunk), chunk)],
+            dst_ref=gath.at[1 + c, core, pl.ds(place * chunk, chunk)],
+            send_sem=psend.at[c, place],
+            recv_sem=precv.at[c, place],
+            device_id={"region": other},
+            device_id_type=MESH,
+        )
+
+    direct = ((0, above), (peers - 1, below), (NEAR, partner))
+
+    def to_partner(c):
+        return pltpu.make_async_remote_copy(
+            src_ref=gath.at[1 + c, core, pl.ds(pl.multiple_of(far * chunk, chunk), chunk)],
+            dst_ref=gath.at[1 + c, core, pl.ds(RELAYED * chunk, chunk)],
+            send_sem=psend.at[c, RELAYED],
+            recv_sem=precv.at[c, RELAYED],
+            device_id={"region": partner},
+            device_id_type=MESH,
+        )
+
+    def arrived(c, place):
+        pltpu.make_async_remote_copy(
+            src_ref=x_ref.at[pl.ds(0, chunk)],
+            dst_ref=gath.at[1 + c, core, pl.ds(pl.multiple_of(place * chunk, chunk), chunk)],
+            send_sem=psend.at[c, place],
+            recv_sem=precv.at[c, place],
+            device_id={"region": partner},
+            device_id_type=MESH,
+        ).wait_recv()
 
     for j in range(1, mp):
         to_core(0, j).start()
-    for s in range(1, slots):
-        to_peer(s).start()
+    for c in range(peers):
+        for place, other in direct:
+            to_peer(place, c, other).start()
     own.wait()
 
+    def pass_on(s):
+        arrived(s - 1, far)
+        to_partner(s - 1).start()
+
     def relay(s):
-        from_peer(s).wait_recv()
+        arrived(s - 1, peers - 1 - far)
+        arrived(s - 1, NEAR)
+        arrived(s - 1, RELAYED)
         for j in range(1, mp):
             to_core(s, j).start()
 
@@ -151,7 +185,8 @@
             nrm[:, cols] = (gath[s, m].astype(jnp.float32) * inv * gain_ref[:, cols]).astype(
                 jnp.bfloat16
             )
-        seen = mask_ref[s]
+        kind = jnp.minimum(s, 1)
+        seen = row_ref[kind]
 
         @pl.when(s == 0)
         def _():
@@ -164,6 +199,12 @@
                 qm[h] = jnp.where(keep, pair, 0.0).astype(jnp.bfloat16)
 
         keys = jnp.dot(nrm[...], w_ref[1], preferred_element_type=jnp.float32)
+
+        @pl.when(s == 0)
+        def _():
+            kown[...] = keys
+
+        keys = jnp.where(column_ref[kind] > 0, keys, kown[...])
         for g in range(heads // 2):
             kbuf[g] = keys[:, g * 2 * HEAD_DIM : (g + 1) * 2 * HEAD_DIM].astype(jnp.bfloat16)
         vals = jnp.dot(nrm[...], w_ref[2], preferred_element_type=jnp.float32)
@@ -174,7 +215,7 @@
             vbuf[h, :HEAD_DIM] = turned[h * HEAD_DIM : (h + 1) * HEAD_DIM].astype(jnp.bfloat16)
             vbuf[h, HEAD_DIM:] = extra
 
-        @pl.when(jnp.logical_and(s >= 1, s < slots - 1))
+        @pl.when(jnp.logical_and(s >= 1, s < blocks - 1))
         def _():
             relay(s + 1)
 
@@ -188,22 +229,32 @@
                 old = top[h]
                 new = jnp.maximum(old, jnp.max(scores, axis=0, keepdims=True))
                 weights = jnp.exp2(scores - new).astype(jnp.bfloat16)
-                scale = jnp.where(seen > 0, jnp.exp2(old - new), 1.0)
-                acc[h] = acc[h] * scale + jnp.dot(
+                acc[h] = acc[h] * jnp.exp2(old - new) + jnp.dot(
                     vbuf[h], weights, preferred_element_type=jnp.float32
                 )
-                top[h] = jnp.where(seen > 0, new, old)
+                top[h] = new
             return carry
 
-        lax.fori_loop(0, heads // 2, two_heads, 0)
+        lax.fori_loop(0, heads // 4, two_heads, 0)
 
         @pl.when(s == 0)
         def _():
+            pass_on(s + 1)
+
+        @pl.when(jnp.logical_and(s >= 1, s < blocks - 2))
+        def _():
+            pass_on(s + 2)
+
+        lax.fori_loop(heads // 4, heads // 2, two_heads, 0)
+
+        @pl.when(s == 0)
+        def _():
             relay(s + 1)
-
-        return carry
-
-    lax.fori_loop(0, slots, block, 0)
+            pass_on(s + 2)
+
+        return carry
+
+    lax.fori_loop(0, blocks, block, 0)
     for h in range(heads):
         mix = acc[h]
         att[h * HEAD_DIM : (h + 1) * HEAD_DIM] = mix[:HEAD_DIM] / mix[HEAD_DIM : HEAD_DIM + 1]
@@ -232,21 +283,24 @@
         total += in_part[j]
     state_ref[...] = total
     back_ref[...] = total.astype(jnp.bfloat16)
-    for s in range(1, slots):
-        to_peer(s).wait_send()
+    for c in range(peers):
+        for place, other in direct:
+            to_peer(place, c, other).wait_send()
+        to_partner(c).wait_send()
 
     def drain(s, carry):
         for j in range(1, mp):
             to_core(s, j).wait_send()
         return carry
 
-    lax.fori_loop(0, slots, drain, 0)
-
-
-def layer(x, gain, w_qkv, w_out, mask, n, mp, cid):
+    lax.fori_loop(0, blocks, drain, 0)
+
+
+def layer(x, gain, w_qkv, w_out, row_mask, column_mask, n, mp, cid):
     rows, width = x.shape
     heads = width // HEAD_DIM
-    slots = len(OFFSETS)
+    peers = PEERS
+    blocks = 1 + peers
     bf16, f32 = jnp.bfloat16, jnp.float32
     vmem = pl.BlockSpec(memory_space=pltpu.VMEM)
     dma = pltpu.SemaphoreType.DMA
@@ -256,12 +310,13 @@
             jax.ShapeDtypeStruct((rows, width), f32),
             jax.ShapeDtypeStruct((rows, width), bf16),
         ),
-        in_specs=[vmem] * 5,
+        in_specs=[vmem] * 6,
         out_specs=(vmem, vmem),
         scratch_shapes=[
-            pltpu.VMEM((slots, mp, rows, width), bf16),
+            pltpu.VMEM((blocks, mp, rows, width), bf16),
             pltpu.VMEM((rows, mp * width), bf16),
             pltpu.VMEM((heads, rows, 2 * HEAD_DIM), bf16),
+            pltpu.VMEM((rows, width), f32),
             pltpu.VMEM((heads // 2, rows, 2 * HEAD_DIM), bf16),
             pltpu.VMEM((heads, PAD, rows), bf16),
             pltpu.VMEM((heads, PAD, rows), f32),
@@ -270,17 +325,17 @@
             pltpu.VMEM((mp, rows, width), f32),
             pltpu.VMEM((mp, rows, width), f32),
             dma,
-            dma((slots,)),
-            dma((slots,)),
-            dma((slots, mp)),
-            dma((slots, mp)),
+            dma((peers, peers)),
+            dma((peers, peers)),
+            dma((blocks, mp)),
+            dma((blocks, mp)),
             dma((mp,)),
             dma((mp,)),
         ],
         compiler_params=pltpu.CompilerParams(
             collective_id=cid, has_side_effects=True, vmem_limit_bytes=56 * 1024 * 1024
         ),
-    )(x, gain, w_qkv, w_out, mask)
+    )(x, gain, w_qkv, w_out, row_mask, column_mask)
 
 
 def on_device(n, mp, grid, g2m_weight, g2m_slot, slot_node, peer_mask, norm_gain, w_qkv, w_out):
@@ -293,20 +348,28 @@
     partial_value = jnp.dot(slot_hot, scaled, preferred_element_type=jnp.float32).astype(
         jnp.bfloat16
     )
-    mesh_in = exchange(partial_value, n, 0)
-    seen = [jnp.ones((1,), jnp.float32)]
-    for column in MASK_COLUMN:
-        seen.append(peer_mask[0, column : column + 1].astype(jnp.float32))
-    mask = jnp.broadcast_to(jnp.concatenate(seen)[:, None, None], (len(OFFSETS), 1, slots))
-    state, back = layer(mesh_in, norm_gain[None, :], w_qkv, w_out, mask, n, mp, 1)
-    returned = exchange(back, n, 2)
+    (mesh_in,) = exchange(partial_value, n, 0)
+    two_below, below, above, two_above = (peer_mask[0, c : c + 1] for c in range(PEERS))
+    odd = lax.axis_index("region") % 2 == 1
+    places = jnp.concatenate(
+        [two_below, jnp.where(odd, below, above), jnp.where(odd, above, below), two_above]
+    )
+    peer_seen = jnp.repeat(places.astype(jnp.float32), slots // PEERS)
+    seen = jnp.stack([jnp.ones_like(peer_seen), peer_seen])
+    state, back = layer(
+        mesh_in, norm_gain[None, :], w_qkv, w_out, seen[:, None, :], seen[:, :, None], n, mp, 1
+    )
     flat_nodes = slot_node[0].reshape(-1)
     node_hot = (jnp.arange(slots, dtype=jnp.int32)[:, None] == flat_nodes[None, :]).astype(
         jnp.bfloat16
     )
-    low = (state - back.astype(jnp.float32)).astype(jnp.bfloat16)
-    mesh_state = jnp.dot(node_hot, back, preferred_element_type=jnp.float32) + jnp.dot(
-        node_hot, low, preferred_element_type=jnp.float32
+    returned, mesh_state = exchange(
+        back,
+        n,
+        2,
+        to_node_order,
+        (state, node_hot),
+        (jax.ShapeDtypeStruct(state.shape, state.dtype),),
     )
     gathered = jnp.dot(slot_hot.T, returned, preferred_element_type=jnp.float32)
     grid_out = (grid.astype(jnp.float32) + gathered).astype(jnp.bfloat16)

time: 122 us -> 114 us (0.934)
  Pallas kernels: 104 us -> 94.4 us
  matrix products: 10.6 us -> 7.64 us
  other arithmetic: 0 us -> 2.35 us
  local copies, waits for them, and re-layouts: 3.03 us -> 4.94 us
    pallas_call x1, Pallas kernels: 64.6 us -> 59.9 us  [layer(): pl.pallas_call(functools.partial(layer_kernel, n, mp), out_shape=(jax.Sha...]
    pallas_call x2, Pallas kernels: 39.1 us -> 34.6 us  [exchange(): pl.pallas_call(functools.partial(exchange_kernel, n, meanwhile), out_shap...]
    dot_general x2 -> x0, matrix products: 4.02 us -> none  [the longest x1 2.48 us: on_device(): jnp.dot(node_hot, low, preferred_element_type=jnp.float32)]
    convert_element_type x0 -> x2, other arithmetic: none -> 2.35 us  [the longest x1 1.41 us: on_device(): peer_seen = jnp.repeat(places.astype(jnp.float32), slots // PEERS)]
where the time goes in v2:
time: 114 us; the launch traced here: 112 us
  Pallas kernels  94.4 us (83%)
  matrix products  7.64 us (7%)
  local copies, waits for them, and re-layouts  4.94 us (4%)
  between operations  3.13 us (3%)
  other arithmetic  2.35 us (2%)
    pallas_call x1, Pallas kernels, layer(): pl.pallas_call(functools.partial(layer_kernel, n, mp), out_shape=(jax.Sha...  59.9 us
    pallas_call x2, Pallas kernels, exchange(): pl.pallas_call(functools.partial(exchange_kernel, n, meanwhile), out_shap...  34.6 us
    dot_general x1, matrix products, on_device(): gathered = jnp.dot(slot_hot.T, returned, preferred_element_type=jnp.float32)  3.91 us
    dot_general x1, matrix products, on_device(): jnp.dot(slot_hot, scaled, preferred_element_type=jnp.float32)  3.73 us

profile of v2, /device:TPU:0, one launch (start us, length us, event | category | flops | bytes accessed | tf_op | source)
XLA Modules:
  0.0 112.5 jit_solution(12410589085702222571)
XLA Ops:
  0.6 0.8 eq.38
  1.4 1.5 %fusion.12 = (s32[1,1]{1,0:T(1,128)}, s32[1,1]{1,0:T(1,128)}, s32[1,1]{1,0:T(1,128)}, s32[1,1]{1,0:T(1,128)}) fusion(s32[1,4]{1,0:T(1,128)} %param.12), kind=kLoop, calls=%fused_computation.15 | loop fusion | bytes 32 | tf_op jit(solution)/shard_map/slice | solution.py:352
  5.3 1.4 %add_convert_fusion = f32[4]{0:T(128)S(1)} fusion(s32[1]{0:T(128)} %bitcast.5, s32[1]{0:T(128)S(6)} %select_n.22, s32[1]{0:T(128)S(6)} %select_n.21, s32[1]{0:T(128)} %bitcast.1), kind=kLoop, calls=%fused_computation.13 | loop fusion | flops 16 | bytes 32 | tf_op jit(solution)/shard_map/convert_element_type | solution.py:357
  6.7 0.1 broadcast_in_dim.17
  6.8 0.6 broadcast_in_dim.18.row_ref
  7.4 1.0 copy.11.column_ref
  8.4 0.9 fusion.11.refs_1_
  9.4 3.7 %fusion.8.x_ref = bf16[512,512]{1,0:T(8,128)(2,1)} fusion(bf16[2048,512]{1,0:T(8,128)(2,1)} %param.8, f32[2048]{0:T(1024)} %param.9, s32[2048]{0:T(1024)} %param.10), kind=kOutput, calls=%fused_computation.10 | convolution fusion | flops 1078198272 | bytes 2637824 | tf_op jit(solution)/shard_map/dot_general | solution.py:348
  13.1 17.5 %shard_map.95.x_ref = bf16[512,512]{1,0:T(8,128)(2,1)} custom-call(bf16[512,512]{1,0:T(8,128)(2,1)} %fusion.8.x_ref), custom_call_target="tpu_custom_call" | custom-call | tf_op jit(solution)/shard_map/pallas_call | solution.py:72
  30.6 0.0 copy-start.1
  30.6 0.0 copy-start.2
  30.6 59.9 %shard_map.96 = (f32[512,512]{1,0:T(8,128)}, bf16[512,512]{1,0:T(8,128)(2,1)}) custom-call(bf16[512,512]{1,0:T(8,128)(2,1)} %shard_map.95.x_ref, f32[1,1024]{1,0:T(1,128)} %bitcast.11, bf16[3,1024,512]{2,1,0:T(8,128)(2,1)} %w_ref.1, bf16[512,1024]{1,0:T(8,128)(2,1)} %wo_ref.1, f32[2,1,512]{2,1,0:T(1,128)} %broadcast_in_dim.18.row_ref, ...), custom_call_target="tpu_custom_call" | custom-call | tf_op jit(solution)/shard_map/pallas_call | solution.py:307
  90.5 17.1 %shard_map.97 = (bf16[512,512]{1,0:T(8,128)(2,1)}, f32[512,512]{1,0:T(8,128)}) custom-call(bf16[512,512]{1,0:T(8,128)(2,1)} %get-tuple-element.6.x_ref, f32[512,512]{1,0:T(8,128)} %get-tuple-element.7.refs_0_, bf16[512,512]{1,0:T(8,128)(2,1)} %fusion.11.refs_1_), custom_call_target="tpu_custom_call" | custom-call | tf_op jit(solution)/shard_map/pallas_call | solution.py:72
  107.6 0.0 copy-done.1
  107.6 0.0 copy-done.2
  107.6 0.0 copy-start
  107.6 3.9 %fusion.1 = bf16[2048,512]{1,0:T(8,128)(2,1)} fusion(bf16[2048,512]{1,0:T(8,128)(2,1)S(1)} %copy-done.1, bf16[512,512]{1,0:T(8,128)(2,1)} %get-tuple-element.9, s32[2048]{0:T(1024)S(1)} %copy-done.2), kind=kOutput, calls=%fused_computation.3 | convolution fusion | flops 1077936128 | bytes 4726784 | tf_op jit(solution)/shard_map/dot_general | solution.py:374
  111.5 0.0 copy-done
  111.5 1.0 copy.13
  (1 shorter events, 0.0 us)
Async XLA Ops:
  30.6 77.0 %copy-start.1 = (bf16[2048,512]{1,0:T(8,128)(2,1)S(1)}, bf16[2048,512]{1,0:T(8,128)(2,1)}, u32[]{:S(2)}) copy-start(bf16[2048,512]{1,0:T(8,128)(2,1)} %param.8) | copy-start | bytes 6291460
  30.6 77.0 %copy-start.2 = (s32[2048]{0:T(1024)S(1)}, s32[2048]{0:T(1024)}, u32[]{:S(2)}) copy-start(s32[2048]{0:T(1024)} %param.10) | copy-start | bytes 24580
  107.6 3.9 %copy-start = (f32[512,512]{1,0:T(8,128)S(1)}, f32[512,512]{1,0:T(8,128)}, u32[]{:S(2)}) copy-start(f32[512,512]{1,0:T(8,128)} %get-tuple-element.18) | copy-start | bytes 3145732
